TPU v7x, 32 devices: a whole 2x2x4 slice. The times are simulated.
32 devices in a mesh: fsdp: 8 (over y, x, core), model: 4 (over z).
Axes of the slice: x: 2, y: 2, z: 4, core: 2. Of those that a mesh axis runs over, the one named last changes fastest.
Arguments:
- w_query: float32 [4096, 4096], P('fsdp', 'model'), may hold values from -0.125 to 0.125
- first_query: float32 [4096, 4096], P('fsdp', 'model'), may hold values from -0.09375 to 0.09375
- second_query: float32 [4096, 4096], P('fsdp', 'model'), may hold values from -0.09375 to 0.09375
- w_key: float32 [4096, 4096], P('fsdp', 'model'), may hold values from -0.125 to 0.125
- first_key: float32 [4096, 4096], P('fsdp', 'model'), may hold values from -0.09375 to 0.09375
- second_key: float32 [4096, 4096], P('fsdp', 'model'), may hold values from -0.09375 to 0.09375
- w_value: float32 [4096, 4096], P('fsdp', 'model'), may hold values from -0.125 to 0.125
- first_value: float32 [4096, 4096], P('fsdp', 'model'), may hold values from -0.09375 to 0.09375
- second_value: float32 [4096, 4096], P('fsdp', 'model'), may hold values from -0.09375 to 0.09375
- norm_gain: float32 [4096], P('fsdp'), may hold values from 0.25 to 1.75
Outputs:
- ready_query: bfloat16 [4096, 4096], P(None, 'model')
- ready_key: bfloat16 [4096, 4096], P(None, 'model')
- ready_value: bfloat16 [4096, 4096], P(None, 'model')
- factor_query: float32 [4096], P('model')
- factor_key: float32 [4096], P('model')
- factor_value: float32 [4096], P('model')
All inputs are finite; a program needn't handle non-finite values. Where the computation divides by a largest or mean magnitude, that divisor is 1e-20 or more.
Results may differ from a plain program's by a relative error of at most 0.001.
Values may be sent and summed in bfloat16 or wider, within the bound.
A program may use at most 128 MiB of HBM per device.

v0:
```python
import jax
import jax.numpy as jnp
from jax import lax
from jax.sharding import PartitionSpec as P

D_MODEL = 4096


learn_rate = 0.2
hold_rate = 0.9


def on_device(
    w_query,
    first_query,
    second_query,
    w_key,
    first_key,
    second_key,
    w_value,
    first_value,
    second_value,
    norm_gain,
):
    hold_query = hold_rate * first_query + second_query
    latest_query = w_query - learn_rate * hold_query
    hold_key = hold_rate * first_key + second_key
    latest_key = w_key - learn_rate * hold_key
    hold_value = hold_rate * first_value + second_value
    latest_value = w_value - learn_rate * hold_value
    latest_gained_query = latest_query * norm_gain[:, None]
    latest_gained_key = latest_key * norm_gain[:, None]
    latest_gained_value = latest_value * norm_gain[:, None]
    total_query, total_key, total_value = lax.psum(
        (
            jnp.sum(jnp.abs(latest_gained_query), axis=0),
            jnp.sum(jnp.abs(latest_gained_key), axis=0),
            jnp.sum(jnp.abs(latest_gained_value), axis=0),
        ),
        "fsdp",
    )
    factor_query = total_query / D_MODEL
    factor_key = total_key / D_MODEL
    factor_value = total_value / D_MODEL
    narrow_query, narrow_key, narrow_value = (
        (latest_gained_query / factor_query).astype(jnp.bfloat16),
        (latest_gained_key / factor_key).astype(jnp.bfloat16),
        (latest_gained_value / factor_value).astype(jnp.bfloat16),
    )
    ready_query, ready_key, ready_value = (
        lax.all_gather(narrow_query, "fsdp", axis=0, tiled=True),
        lax.all_gather(narrow_key, "fsdp", axis=0, tiled=True),
        lax.all_gather(narrow_value, "fsdp", axis=0, tiled=True),
    )
    return (ready_query, ready_key, ready_value, factor_query, factor_key, factor_value)


def solution(mesh):
    return jax.shard_map(
        on_device,
        mesh=mesh,
        in_specs=(
            P("fsdp", "model"),
            P("fsdp", "model"),
            P("fsdp", "model"),
            P("fsdp", "model"),
            P("fsdp", "model"),
            P("fsdp", "model"),
            P("fsdp", "model"),
            P("fsdp", "model"),
            P("fsdp", "model"),
            P("fsdp"),
        ),
        out_specs=(
            P(None, "model"),
            P(None, "model"),
            P(None, "model"),
            P("model"),
            P("model"),
            P("model"),
        ),
        check_vma=False,
    )
```

profile of v0, /device:TPU:0, one launch (start us, length us, event | category | flops | bytes accessed | tf_op | source)
XLA Modules:
  0.0 242.5 jit_solution(16033579004505762877)
XLA Ops:
  7.2 0.0 all-gather.4.cloned.1.call-start
  7.2 9.8 %abs_reduce_fusion = (f32[1024]{0:T(1024)S(1)}, f32[512,1024]{1,0:T(8,128)S(1)}, f32[1024]{0:T(1024)S(1)}, f32[512,1024]{1,0:T(8,128)}, f32[1024]{0:T(1024)S(1)}, /*index=5*/f32[512,1024]{1,0:T(8,128)}) fusion(f32[512]{0:T(512)} %param.19, f32[512,1024]{1,0:T(8,128)} %param.16, f32[512,1024]{1,0:T(8,128)} %param.18, f32[512,1024]{1,0:T(8,128)} %param.17, ...), kind=kLoop, calls=%fused_computation.1 | loop fusion | flops 11006976 | bytes 25180160 | tf_op jit(solution)/shard_map/reduce_sum | solution.py:38
  17.1 25.5 %all-reduce = (f32[1024]{0:T(1024)S(1)}, f32[1024]{0:T(1024)S(1)}, f32[1024]{0:T(1024)S(1)}) all-reduce(f32[1024]{0:T(1024)S(1)} %get-tuple-element.17, f32[1024]{0:T(1024)S(1)} %get-tuple-element.15, f32[1024]{0:T(1024)S(1)} %get-tuple-element.9), channel_id=1, replica_groups=mesh['fsdp'=8,'model'=4] {'fsdp'}, use_global_device_ids=true, to_apply=%region_1.0 | all-reduce | flops 3072 | bytes 24576 | tf_op jit(solution)/shard_map/psum | solution.py:34
  42.6 0.0 copy-start
  42.6 2.8 %divide_convert_fusion.2 = bf16[512,1024]{1,0:T(8,128)(2,1)} fusion(f32[512,1024]{1,0:T(8,128)} %get-tuple-element.18, f32[1024]{0:T(1024)S(1)} %broadcast_multiply_fusion.2), kind=kLoop, calls=%fused_computation.6 | loop fusion | flops 1048576 | bytes 3149824 | tf_op jit(solution)/shard_map/convert_element_type | solution.py:46
  45.4 0.0 all-gather.4.cloned.1.call-update
  45.4 0.0 copy-done
  45.4 0.0 all-gather.6.cloned.1.call-start
  45.5 0.0 copy-start.1
  45.5 2.8 %divide_convert_fusion.1 = bf16[512,1024]{1,0:T(8,128)(2,1)} fusion(f32[512,1024]{1,0:T(8,128)} %get-tuple-element.16, f32[1024]{0:T(1024)S(1)} %broadcast_multiply_fusion.1), kind=kLoop, calls=%fused_computation.3 | loop fusion | flops 1048576 | bytes 3149824 | tf_op jit(solution)/shard_map/convert_element_type | solution.py:47
  48.3 0.0 all-gather.6.cloned.1.call-update
  48.4 0.0 copy-done.1
  48.4 0.0 all-gather.8.cloned.1.call-start
  48.4 0.0 copy-start.2
  48.4 1.2 divide_convert_fusion
  49.7 0.0 all-gather.8.cloned.1.call-update
  49.7 0.0 copy-done.2
  49.7 49.5 %all-gather.4.cloned.1.call-done = bf16[4096,1024]{1,0:T(8,128)(2,1)} async-done(((bf16[512,1024]{1,0:T(8,128)(2,1)}), bf16[4096,1024]{1,0:T(8,128)(2,1)}) %all-gather.4.cloned.1.call-update) | async-done | bytes 8388624 | tf_op jit(solution)/shard_map/all_gather | solution.py:51
  99.2 56.7 %all-gather.6.cloned.1.call-done = bf16[4096,1024]{1,0:T(8,128)(2,1)} async-done(((bf16[512,1024]{1,0:T(8,128)(2,1)}), bf16[4096,1024]{1,0:T(8,128)(2,1)}) %all-gather.6.cloned.1.call-update) | async-done | bytes 8388624 | tf_op jit(solution)/shard_map/all_gather | solution.py:52
  156.0 56.8 %all-gather.8.cloned.1.call-done = bf16[4096,1024]{1,0:T(8,128)(2,1)} async-done(((bf16[512,1024]{1,0:T(8,128)(2,1)}), bf16[4096,1024]{1,0:T(8,128)(2,1)}) %all-gather.8.cloned.1.call-update) | async-done | bytes 8388624 | tf_op jit(solution)/shard_map/all_gather | solution.py:53
  212.7 7.8 %copy.19 = bf16[4096,1024]{1,0:T(8,128)(2,1)} copy(bf16[4096,1024]{1,0:T(8,128)(2,1)} %all-gather.4.cloned.1.call-done) | data formatting | bytes 16777216
  220.5 7.8 %copy.20 = bf16[4096,1024]{1,0:T(8,128)(2,1)} copy(bf16[4096,1024]{1,0:T(8,128)(2,1)} %all-gather.6.cloned.1.call-done) | data formatting | bytes 16777216
  228.2 7.8 %copy.21 = bf16[4096,1024]{1,0:T(8,128)(2,1)} copy(bf16[4096,1024]{1,0:T(8,128)(2,1)} %all-gather.8.cloned.1.call-done) | data formatting | bytes 16777216
  (3 shorter events, 0.0 us)
Async XLA Ops:
  7.2 92.0 %all-gather.4.cloned.1.call-start = ((), (), s32[]{:S(2)}) async-start(), calls=%async_computation | async-start | bytes 9437184 | tf_op jit(solution)/shard_map/all_gather | solution.py:51
  42.6 2.8 %copy-start = (f32[1024]{0:T(1024)}, f32[1024]{0:T(1024)S(1)}, u32[]{:S(2)}) copy-start(f32[1024]{0:T(1024)S(1)} %broadcast_multiply_fusion.2) | copy-start | bytes 12292
  45.4 110.5 %all-gather.6.cloned.1.call-start = ((), (), s32[]{:S(2)}) async-start(), calls=%async_computation.1 | async-start | bytes 9437184 | tf_op jit(solution)/shard_map/all_gather | solution.py:52
  45.5 2.9 %copy-start.1 = (f32[1024]{0:T(1024)}, f32[1024]{0:T(1024)S(1)}, u32[]{:S(2)}) copy-start(f32[1024]{0:T(1024)S(1)} %broadcast_multiply_fusion.1) | copy-start | bytes 12292
  48.4 164.3 %all-gather.8.cloned.1.call-start = ((), (), s32[]{:S(2)}) async-start(), calls=%async_computation.2 | async-start | bytes 9437184 | tf_op jit(solution)/shard_map/all_gather | solution.py:53
  48.4 1.3 copy-start.2
Sparse Core Ops, SparseCore 0:
  45.6 53.6 all-gather.3
  101.7 54.2 all-gather.5
  158.4 54.2 all-gather.7
where the time goes:
time: 243 us
  waiting for transfers between devices  163 us (67%)
  blocking collectives  25.5 us (10%)
  local copies, waits for them, and re-layouts  23.3 us (10%)
  other arithmetic  16.7 us (7%)
  between operations  13.8 us (6%)
    all_gather x1, waiting for transfers between devices, on_device(): lax.all_gather(narrow_value, 'fsdp', axis=0, tiled=True)  56.8 us
    all_gather x1, waiting for transfers between devices, on_device(): lax.all_gather(narrow_key, 'fsdp', axis=0, tiled=True)  56.7 us
    all_gather x1, waiting for transfers between devices, on_device(): lax.all_gather(narrow_query, 'fsdp', axis=0, tiled=True)  49.5 us
    psum x1, blocking collectives, on_device(): lax.psum((jnp.sum(jnp.abs(latest_gained_query), axis=0), jnp.sum(jnp.abs(...  25.5 us
    unnamed x9, local copies, waits for them, and re-layouts  23.3 us
    reduce_sum x1, other arithmetic, on_device(): jnp.sum(jnp.abs(latest_gained_value), axis=0)  9.84 us
  transfers between devices with their start and end apart: 3, of which 3 were waited for; matrix products, arithmetic and copies ran while one was open for 2% of the time, Pallas kernels for 0%

commit v1 on v0

v1 whole, which is shorter than its diff:
```python
import functools
import math

import jax
import jax.numpy as jnp
from jax import lax
from jax.experimental import pallas as pl
from jax.experimental.pallas import tpu as pltpu
from jax.sharding import PartitionSpec as P

learn_rate = 0.2
hold_rate = 0.9
MESH = pl.DeviceIdType.MESH
UNITS = 2
STEP = 32


def plain(
    w_query,
    first_query,
    second_query,
    w_key,
    first_key,
    second_key,
    w_value,
    first_value,
    second_value,
    norm_gain,
    rows,
):
    gained = []
    for w, first, second in (
        (w_query, first_query, second_query),
        (w_key, first_key, second_key),
        (w_value, first_value, second_value),
    ):
        hold = hold_rate * first + second
        gained.append((w - learn_rate * hold) * norm_gain[:, None])
    totals = lax.psum(tuple(jnp.sum(jnp.abs(g), axis=0) for g in gained), "fsdp")
    factors = tuple(t / rows for t in totals)
    ready = tuple(
        lax.all_gather(
            (g / f).astype(jnp.bfloat16), "fsdp", axis=0, tiled=True
        )
        for g, f in zip(gained, factors)
    )
    return ready + factors


def gather_kernel(total_rows, *refs):
    ins, gain_ref = refs[:9], refs[9]
    outs, factor_ref = refs[10:13], refs[13]
    (
        w_buf, first_buf, second_buf, gain_buf, mine, parts,
        load_sem, sum_send, sum_recv, x_recv, y_recv, diag_recv,
        chip_recv, send_sem,
    ) = refs[14:]
    bufs = (w_buf, first_buf, second_buf)
    rows, cols = w_buf.shape[1:]
    width = cols // UNITS
    half = rows // 2

    me = lax.axis_index("fsdp")
    core = me % 2
    x = (me // 2) % 2
    y = me // 4
    partner = me + 1 - 2 * core
    x_near = me + 2 - 4 * x
    y_near = me + 4 - 8 * y
    diag = x_near + 4 - 8 * y
    peers = [
        partner, x_near, y_near, diag,
        x_near + 1 - 2 * core, y_near + 1 - 2 * core, diag + 1 - 2 * core,
    ]

    units = [(m, c) for m in range(3) for c in range(UNITS)]
    loads = []
    for u, (m, c) in enumerate(units):
        at = pl.ds(c * width, width)
        loads.append([
            pltpu.make_async_copy(
                ins[3 * m + k].at[:, at], bufs[k].at[m, :, at], load_sem.at[u, k]
            )
            for k in range(3)
        ])
    for group in loads:
        for copy in group:
            copy.start()

    barrier = pltpu.get_barrier_semaphore()
    for peer in peers:
        pl.semaphore_signal(
            barrier, inc=1, device_id={"fsdp": peer}, device_id_type=MESH
        )

    for k in range(rows // 128):
        line = gain_ref[:, pl.ds(k * 128, 128)]
        gain_buf[pl.ds(k * 128, 128), :] = jnp.broadcast_to(line, (128, 128)).T

    def sums(u):
        m, c = units[u]
        for copy in loads[u]:
            copy.wait()
        tiles = width // 128

        def body(i, acc):
            at = pl.ds(pl.multiple_of(i * STEP, STEP), STEP)
            gain = gain_buf[at, :]
            new = []
            for t in range(tiles):
                lanes = pl.ds(c * width + t * 128, 128)
                hold = hold_rate * first_buf[m, at, lanes] + second_buf[m, at, lanes]
                gained = (w_buf[m, at, lanes] - learn_rate * hold) * gain
                w_buf[m, at, lanes] = gained
                size = jnp.abs(gained)
                new.append(
                    acc[t] + jnp.sum(size.reshape(STEP // 8, 8, 128), axis=0)
                )
            return tuple(new)

        acc = lax.fori_loop(
            0, rows // STEP, body,
            tuple(jnp.zeros((8, 128), jnp.float32) for _ in range(tiles)),
        )
        for t in range(tiles):
            mine[u, :, pl.ds(t * 128, 128)] = jnp.sum(acc[t], axis=0, keepdims=True)

    def sum_copy(u, slot, peer):
        return pltpu.make_async_remote_copy(
            src_ref=mine.at[u],
            dst_ref=parts.at[u, slot],
            send_sem=sum_send.at[u, slot],
            recv_sem=sum_recv.at[u, slot],
            device_id={"fsdp": peer},
            device_id_type=MESH,
        )

    def send_sums(u):
        for slot, peer in enumerate(peers):
            sum_copy(u, slot, peer).start()

    def block(m, c, owner, first, count):
        at = pl.ds(pl.multiple_of(owner * rows + first, 16), count)
        return outs[m].at[at, pl.ds(c * width, width)]

    def send(m, ref, recv_sem, peer):
        pltpu.make_async_remote_copy(
            src_ref=ref, dst_ref=ref, send_sem=send_sem.at[m], recv_sem=recv_sem,
            device_id={"fsdp": peer}, device_id_type=MESH,
        ).start()

    def arrived(ref, recv_sem):
        pltpu.make_async_remote_copy(
            src_ref=ref, dst_ref=ref, send_sem=send_sem.at[0], recv_sem=recv_sem,
            device_id={"fsdp": partner}, device_id_type=MESH,
        ).wait_recv()

    def finish(u):
        m, c = units[u]
        for slot, peer in enumerate(peers):
            sum_copy(u, slot, peer).wait_recv()
        total = mine[u]
        for slot in range(7):
            total = total + parts[u, slot]
        factor = total / total_rows
        factor_ref[pl.ds(m, 1), pl.ds(c * width, width)] = factor
        scale = jnp.broadcast_to(1.0 / factor, (16, width))

        def body(i, carry):
            for k in range(STEP // 16):
                at = pl.multiple_of(i * STEP + k * 16, 16)
                tile = w_buf[m, pl.ds(at, 16), pl.ds(c * width, width)] * scale
                outs[m][
                    pl.ds(pl.multiple_of(me * rows + at, 16), 16),
                    pl.ds(c * width, width),
                ] = tile.astype(jnp.bfloat16)
            return carry

        for h in range(2):
            lo = h * half // STEP
            lax.fori_loop(lo, lo + half // STEP, body, 0)
            ref = block(m, c, me, h * half, half)
            send(m, ref, x_recv.at[u, h], x_near)
            send(m, ref, y_recv.at[u, h], y_near)
        send(m, block(m, c, me, 0, rows), chip_recv.at[m], partner)

    count = len(units)
    for u in range(count):
        sums(u)
        if u == 0:
            pl.semaphore_wait(barrier, 7)
        send_sums(u)
        if u >= 1:
            finish(u - 1)
    finish(count - 1)

    for u, (m, c) in enumerate(units):
        for h in range(2):
            ref = block(m, c, x_near, h * half, half)
            arrived(ref, x_recv.at[u, h])
            if h == 0:
                send(m, ref, diag_recv.at[u, 0], y_near)
            send(m, ref, chip_recv.at[m], partner)
            ref = block(m, c, y_near, h * half, half)
            arrived(ref, y_recv.at[u, h])
            if h == 1:
                send(m, ref, diag_recv.at[u, 1], x_near)
            send(m, ref, chip_recv.at[m], partner)
    for u, (m, c) in enumerate(units):
        for h in range(2):
            ref = block(m, c, diag, h * half, half)
            arrived(ref, diag_recv.at[u, h])
            send(m, ref, chip_recv.at[m], partner)

    for m in range(3):
        taken = outs[m].at[pl.ds(0, 4 * rows), :]
        sent = outs[m].at[pl.ds(0, 7 * rows), :]
        arrived(taken, chip_recv.at[m])
        pltpu.make_async_remote_copy(
            src_ref=sent, dst_ref=sent, send_sem=send_sem.at[m],
            recv_sem=chip_recv.at[m], device_id={"fsdp": partner},
            device_id_type=MESH,
        ).wait_send()
    for u in range(count):
        for slot, peer in enumerate(peers):
            sum_copy(u, slot, peer).wait_send()


def write_kernel(a, b, c, factor, out_a, out_b, out_c, fa, fb, fc, sem):
    copies = []
    for k, (src, dst) in enumerate(((a, out_a), (b, out_b), (c, out_c))):
        rows = src.shape[0] // 4
        for p in range(4):
            at = pl.ds(p * rows, rows)
            copies.append(
                pltpu.make_async_copy(src.at[at, :], dst.at[at, :], sem.at[k, p])
            )
    for copy in copies:
        copy.start()
    for m, out in enumerate((fa, fb, fc)):
        out[...] = factor[m, :]
    for copy in copies:
        copy.wait()


def ringed(*args, total_rows):
    rows, cols = args[0].shape
    count = 3 * UNITS
    width = cols // UNITS
    big = (8 * rows, cols)
    vmem = pl.BlockSpec(memory_space=pltpu.VMEM)
    hbm = pl.BlockSpec(memory_space=pltpu.HBM)
    buf = pltpu.VMEM((3, rows, cols), jnp.float32)
    dma = pltpu.SemaphoreType.DMA
    *gathered, factor = pl.pallas_call(
        functools.partial(gather_kernel, total_rows),
        out_shape=[pltpu.VMEM(big, jnp.bfloat16)] * 3
        + [pltpu.VMEM((3, cols), jnp.float32)],
        in_specs=[hbm] * 9 + [vmem],
        out_specs=[vmem] * 4,
        scratch_shapes=[
            buf, buf, buf,
            pltpu.VMEM((rows, 128), jnp.float32),
            pltpu.VMEM((count, 1, width), jnp.float32),
            pltpu.VMEM((count, 7, 1, width), jnp.float32),
            dma((count, 3)),
            dma((count, 7)), dma((count, 7)),
            dma((count, 2)), dma((count, 2)), dma((count, 2)),
            dma((3,)), dma((3,)),
        ],
        compiler_params=pltpu.CompilerParams(
            collective_id=0, has_side_effects=True,
            vmem_limit_bytes=24 * 2**20,
        ),
        name="gather",
    )(*args[:9], args[9].reshape(1, rows))
    ready = jax.ShapeDtypeStruct(big, jnp.bfloat16)
    line = jax.ShapeDtypeStruct((cols,), jnp.float32)
    return pl.pallas_call(
        write_kernel,
        out_shape=[ready] * 3 + [line] * 3,
        in_specs=[vmem] * 4,
        out_specs=[hbm] * 3 + [vmem] * 3,
        scratch_shapes=[dma((3, 4))],
        compiler_params=pltpu.CompilerParams(vmem_limit_bytes=2**20),
        name="write",
    )(*gathered, factor)


def on_device(*args, devices):
    rows, cols = args[0].shape
    total_rows = devices * rows
    fits = rows * cols * (36 + 48) <= 48 * 2**20
    if devices == 8 and rows % 128 == 0 and cols % (128 * UNITS) == 0 and fits:
        return tuple(ringed(*args, total_rows=total_rows))
    return plain(*args, rows=total_rows)


def solution(mesh):
    return jax.shard_map(
        functools.partial(on_device, devices=mesh.shape["fsdp"]),
        mesh=mesh,
        in_specs=(P("fsdp", "model"),) * 9 + (P("fsdp"),),
        out_specs=(P(None, "model"),) * 3 + (P("model"),) * 3,
        check_vma=False,
    )
```

time: 243 us -> 128 us (0.53)
  waiting for transfers between devices: 163 us -> 0 us
  Pallas kernels: 0 us -> 123 us
  blocking collectives: 25.5 us -> 0 us
  local copies, waits for them, and re-layouts: 23.3 us -> 3.86 us
  other arithmetic: 16.7 us -> 0 us
  between operations: 13.8 us -> 0.65 us
    all_gather x3 -> x0, waiting for transfers between devices: 163 us -> none  [the longest x1 56.8 us: on_device(): lax.all_gather(narrow_value, 'fsdp', axis=0, tiled=True)]
    pallas_call x0 -> x2, Pallas kernels: none -> 123 us  [the longest x1 114 us: ringed(): pl.pallas_call(functools.partial(gather_kernel, total_rows), out_shape=[p...]
    psum x1 -> x0, blocking collectives: 25.5 us -> none  [on_device(): lax.psum((jnp.sum(jnp.abs(latest_gained_query), axis=0), jnp.sum(jnp.abs(...]
    unnamed x9 -> x6, local copies, waits for them, and re-layouts: 23.3 us -> 3.86 us
    reduce_sum x1 -> x0, other arithmetic: 9.84 us -> none  [on_device(): jnp.sum(jnp.abs(latest_gained_value), axis=0)]
    convert_element_type x3 -> x0, other arithmetic: 6.87 us -> none  [the longest x1 2.82 us: on_device(): (latest_gained_query / factor_query).astype(jnp.bfloat16)]
  transfers between devices with their start and end apart: 3 -> 0, of which waited for: 3 -> 0; matrix products, arithmetic and copies ran while one was open for 2% -> 0% of each run, Pallas kernels for 0% -> 0%
where the time goes in v1:
time: 128 us
  Pallas kernels  123 us (96%)
  local copies, waits for them, and re-layouts  3.86 us (3%)
    pallas_call x1, Pallas kernels, ringed(): pl.pallas_call(functools.partial(gather_kernel, total_rows), out_shape=[p...  114 us
    pallas_call x1, Pallas kernels, ringed(): pl.pallas_call(write_kernel, out_shape=[ready] * 3 + [line] * 3, in_specs...  9.08 us
    unnamed x6, local copies, waits for them, and re-layouts  3.86 us

profile of v1, /device:TPU:0, one launch (start us, length us, event | category | flops | bytes accessed | tf_op | source)
XLA Modules:
  0.0 128.0 jit_solution(4527314250102473570)
XLA Ops:
  0.6 0.0 copy-start
  0.6 1.6 %copy-done = f32[512,1024]{1,0:T(8,128)S(1)} copy-done((f32[512,1024]{1,0:T(8,128)S(1)}, f32[512,1024]{1,0:T(8,128)}, u32[]{:S(2)}) %copy-start) | copy-done | bytes 2097176
  2.2 0.0 copy-start.1
  2.2 1.6 %copy-done.1 = f32[512,1024]{1,0:T(8,128)S(1)} copy-done((f32[512,1024]{1,0:T(8,128)S(1)}, f32[512,1024]{1,0:T(8,128)}, u32[]{:S(2)}) %copy-start.1) | copy-done | bytes 2097176
  3.8 0.0 copy-start.2
  3.8 0.7 copy-done.2
  4.5 114.4 %gather.1 = (bf16[4096,1024]{1,0:T(8,128)(2,1)S(1)}, bf16[4096,1024]{1,0:T(8,128)(2,1)S(1)}, bf16[4096,1024]{1,0:T(8,128)(2,1)S(1)}, f32[3,1024]{1,0:T(4,128)S(1)}) custom-call(f32[512,1024]{1,0:T(8,128)S(1)} %copy-done, f32[512,1024]{1,0:T(8,128)S(1)} %copy-done.1, f32[512,1024]{1,0:T(8,128)} %refs_2_.1, f32[512,1024]{1,0:T(8,128)} %refs_3_.1, ...), custom_call_target="tpu_custom_call" | custom-call | tf_op jit(solution)/shard_map/gather/pallas_call | solution.py:255
  118.9 9.1 %write.1 = (bf16[4096,1024]{1,0:T(8,128)(2,1)}, bf16[4096,1024]{1,0:T(8,128)(2,1)}, bf16[4096,1024]{1,0:T(8,128)(2,1)}, f32[1024]{0:T(1024)}, f32[1024]{0:T(1024)}, /*index=5*/f32[1024]{0:T(1024)}) custom-call(bf16[4096,1024]{1,0:T(8,128)(2,1)S(1)} %get-tuple-element.10.a, bf16[4096,1024]{1,0:T(8,128)(2,1)S(1)} %get-tuple-element.11.b, ...), custom_call_target="tpu_custom_call" | custom-call | tf_op jit(solution)/shard_map/write/pallas_call | solution.py:279
Async XLA Ops:
  0.6 1.6 %copy-start = (f32[512,1024]{1,0:T(8,128)S(1)}, f32[512,1024]{1,0:T(8,128)}, u32[]{:S(2)}) copy-start(f32[512,1024]{1,0:T(8,128)} %refs_0_.1) | copy-start | bytes 6291460
  2.2 1.6 %copy-start.1 = (f32[512,1024]{1,0:T(8,128)S(1)}, f32[512,1024]{1,0:T(8,128)}, u32[]{:S(2)}) copy-start(f32[512,1024]{1,0:T(8,128)} %refs_1_.1) | copy-start | bytes 6291460
  3.8 0.7 copy-start.2

commit v2 on v1

--- a/solution.py
+++ b/solution.py
@@ -11,8 +11,11 @@
 learn_rate = 0.2
 hold_rate = 0.9
 MESH = pl.DeviceIdType.MESH
-UNITS = 2
+UNITS = 4
+PARTS = ((1, 1, 2), (2, 2), (2, 1, 1))
 STEP = 32
+AHEAD = 2
+VMEM_BYTES = 67_043_328
 
 
 def plain(
@@ -47,17 +50,26 @@
     return ready + factors
 
 
+def units_of(cols):
+    units = []
+    for m, sizes in enumerate(PARTS):
+        first = 0
+        for size in sizes:
+            units.append((m, first, size * cols // UNITS))
+            first += size * cols // UNITS
+    return units
+
+
 def gather_kernel(total_rows, *refs):
     ins, gain_ref = refs[:9], refs[9]
     outs, factor_ref = refs[10:13], refs[13]
     (
-        w_buf, first_buf, second_buf, gain_buf, mine, parts,
-        load_sem, sum_send, sum_recv, x_recv, y_recv, diag_recv,
+        w_buf, first_buf, second_buf, gain_line, gain_buf, mine, parts,
+        load_sem, gain_sem, sum_send, sum_recv, x_recv, y_recv, diag_recv,
         chip_recv, send_sem,
     ) = refs[14:]
     bufs = (w_buf, first_buf, second_buf)
     rows, cols = w_buf.shape[1:]
-    width = cols // UNITS
     half = rows // 2
 
     me = lax.axis_index("fsdp")
@@ -73,19 +85,26 @@
         x_near + 1 - 2 * core, y_near + 1 - 2 * core, diag + 1 - 2 * core,
     ]
 
-    units = [(m, c) for m in range(3) for c in range(UNITS)]
+    units = units_of(cols)
     loads = []
-    for u, (m, c) in enumerate(units):
-        at = pl.ds(c * width, width)
+    for u, (m, c, width) in enumerate(units):
+        at = pl.ds(c, width)
         loads.append([
             pltpu.make_async_copy(
                 ins[3 * m + k].at[:, at], bufs[k].at[m, :, at], load_sem.at[u, k]
             )
             for k in range(3)
         ])
-    for group in loads:
-        for copy in group:
-            copy.start()
+
+    def load(u):
+        if u < len(units):
+            for copy in loads[u]:
+                copy.start()
+
+    gain_copy = pltpu.make_async_copy(gain_ref, gain_line, gain_sem)
+    gain_copy.start()
+    for u in range(AHEAD):
+        load(u)
 
     barrier = pltpu.get_barrier_semaphore()
     for peer in peers:
@@ -93,14 +112,16 @@
             barrier, inc=1, device_id={"fsdp": peer}, device_id_type=MESH
         )
 
+    gain_copy.wait()
     for k in range(rows // 128):
-        line = gain_ref[:, pl.ds(k * 128, 128)]
+        line = gain_line[:, pl.ds(k * 128, 128)]
         gain_buf[pl.ds(k * 128, 128), :] = jnp.broadcast_to(line, (128, 128)).T
 
     def sums(u):
-        m, c = units[u]
+        m, c, width = units[u]
         for copy in loads[u]:
             copy.wait()
+        load(u + AHEAD)
         tiles = width // 128
 
         def body(i, acc):
@@ -108,7 +129,7 @@
             gain = gain_buf[at, :]
             new = []
             for t in range(tiles):
-                lanes = pl.ds(c * width + t * 128, 128)
+                lanes = pl.ds(c + t * 128, 128)
                 hold = hold_rate * first_buf[m, at, lanes] + second_buf[m, at, lanes]
                 gained = (w_buf[m, at, lanes] - learn_rate * hold) * gain
                 w_buf[m, at, lanes] = gained
@@ -127,8 +148,8 @@
 
     def sum_copy(u, slot, peer):
         return pltpu.make_async_remote_copy(
-            src_ref=mine.at[u],
-            dst_ref=parts.at[u, slot],
+            src_ref=mine.at[u, :, pl.ds(0, units[u][2])],
+            dst_ref=parts.at[u, slot, :, pl.ds(0, units[u][2])],
             send_sem=sum_send.at[u, slot],
             recv_sem=sum_recv.at[u, slot],
             device_id={"fsdp": peer},
@@ -139,9 +160,10 @@
         for slot, peer in enumerate(peers):
             sum_copy(u, slot, peer).start()
 
-    def block(m, c, owner, first, count):
+    def block(u, owner, first, count):
+        m, c, width = units[u]
         at = pl.ds(pl.multiple_of(owner * rows + first, 16), count)
-        return outs[m].at[at, pl.ds(c * width, width)]
+        return outs[m].at[at, pl.ds(c, width)]
 
     def send(m, ref, recv_sem, peer):
         pltpu.make_async_remote_copy(
@@ -156,33 +178,33 @@
         ).wait_recv()
 
     def finish(u):
-        m, c = units[u]
+        m, c, width = units[u]
         for slot, peer in enumerate(peers):
             sum_copy(u, slot, peer).wait_recv()
-        total = mine[u]
+        total = mine[u, :, pl.ds(0, width)]
         for slot in range(7):
-            total = total + parts[u, slot]
+            total = total + parts[u, slot, :, pl.ds(0, width)]
         factor = total / total_rows
-        factor_ref[pl.ds(m, 1), pl.ds(c * width, width)] = factor
+        factor_ref[pl.ds(m, 1), pl.ds(c, width)] = factor
         scale = jnp.broadcast_to(1.0 / factor, (16, width))
 
         def body(i, carry):
             for k in range(STEP // 16):
                 at = pl.multiple_of(i * STEP + k * 16, 16)
-                tile = w_buf[m, pl.ds(at, 16), pl.ds(c * width, width)] * scale
+                tile = w_buf[m, pl.ds(at, 16), pl.ds(c, width)] * scale
                 outs[m][
                     pl.ds(pl.multiple_of(me * rows + at, 16), 16),
-                    pl.ds(c * width, width),
+                    pl.ds(c, width),
                 ] = tile.astype(jnp.bfloat16)
             return carry
 
         for h in range(2):
             lo = h * half // STEP
             lax.fori_loop(lo, lo + half // STEP, body, 0)
-            ref = block(m, c, me, h * half, half)
+            ref = block(u, me, h * half, half)
             send(m, ref, x_recv.at[u, h], x_near)
             send(m, ref, y_recv.at[u, h], y_near)
-        send(m, block(m, c, me, 0, rows), chip_recv.at[m], partner)
+        send(m, block(u, me, 0, rows), chip_recv.at[m], partner)
 
     count = len(units)
     for u in range(count):
@@ -194,21 +216,21 @@
             finish(u - 1)
     finish(count - 1)
 
-    for u, (m, c) in enumerate(units):
+    for u, (m, _, _) in enumerate(units):
         for h in range(2):
-            ref = block(m, c, x_near, h * half, half)
+            ref = block(u, x_near, h * half, half)
             arrived(ref, x_recv.at[u, h])
             if h == 0:
                 send(m, ref, diag_recv.at[u, 0], y_near)
             send(m, ref, chip_recv.at[m], partner)
-            ref = block(m, c, y_near, h * half, half)
+            ref = block(u, y_near, h * half, half)
             arrived(ref, y_recv.at[u, h])
             if h == 1:
                 send(m, ref, diag_recv.at[u, 1], x_near)
             send(m, ref, chip_recv.at[m], partner)
-    for u, (m, c) in enumerate(units):
+    for u, (m, _, _) in enumerate(units):
         for h in range(2):
-            ref = block(m, c, diag, h * half, half)
+            ref = block(u, diag, h * half, half)
             arrived(ref, diag_recv.at[u, h])
             send(m, ref, chip_recv.at[m], partner)
 
@@ -245,8 +267,9 @@
 
 def ringed(*args, total_rows):
     rows, cols = args[0].shape
-    count = 3 * UNITS
-    width = cols // UNITS
+    units = units_of(cols)
+    count = len(units)
+    width = max(unit[2] for unit in units)
     big = (8 * rows, cols)
     vmem = pl.BlockSpec(memory_space=pltpu.VMEM)
     hbm = pl.BlockSpec(memory_space=pltpu.HBM)
@@ -256,24 +279,28 @@
         functools.partial(gather_kernel, total_rows),
         out_shape=[pltpu.VMEM(big, jnp.bfloat16)] * 3
         + [pltpu.VMEM((3, cols), jnp.float32)],
-        in_specs=[hbm] * 9 + [vmem],
+        in_specs=[hbm] * 10,
         out_specs=[vmem] * 4,
         scratch_shapes=[
             buf, buf, buf,
+            pltpu.VMEM((1, rows), jnp.float32),
             pltpu.VMEM((rows, 128), jnp.float32),
             pltpu.VMEM((count, 1, width), jnp.float32),
             pltpu.VMEM((count, 7, 1, width), jnp.float32),
-            dma((count, 3)),
+            dma((count, 3)), dma,
             dma((count, 7)), dma((count, 7)),
             dma((count, 2)), dma((count, 2)), dma((count, 2)),
             dma((3,)), dma((3,)),
         ],
         compiler_params=pltpu.CompilerParams(
             collective_id=0, has_side_effects=True,
-            vmem_limit_bytes=24 * 2**20,
+            vmem_limit_bytes=VMEM_BYTES - 3 * 16 * rows * cols - 2**20,
         ),
         name="gather",
-    )(*args[:9], args[9].reshape(1, rows))
+    )(*(
+        pltpu.with_memory_space_constraint(a, pltpu.HBM)
+        for a in (*args[:9], args[9].reshape(1, rows))
+    ))
     ready = jax.ShapeDtypeStruct(big, jnp.bfloat16)
     line = jax.ShapeDtypeStruct((cols,), jnp.float32)
     return pl.pallas_call(

time: 128 us -> 124 us (0.969)
  local copies, waits for them, and re-layouts: 3.86 us -> 0 us
    unnamed x6 -> x0, local copies, waits for them, and re-layouts: 3.86 us -> none
where the time goes in v2:
time: 124 us
  Pallas kernels  123 us (99%)
    pallas_call x1, Pallas kernels, ringed(): pl.pallas_call(functools.partial(gather_kernel, total_rows), out_shape=[p...  114 us
    pallas_call x1, Pallas kernels, ringed(): pl.pallas_call(write_kernel, out_shape=[ready] * 3 + [line] * 3, in_specs...  9.08 us

profile of v2, /device:TPU:0, one launch (start us, length us, event | category | flops | bytes accessed | tf_op | source)
XLA Modules:
  0.0 123.7 jit_solution(394601932589446835)
XLA Ops:
  0.6 114.0 %gather.1 = (bf16[4096,1024]{1,0:T(8,128)(2,1)S(1)}, bf16[4096,1024]{1,0:T(8,128)(2,1)S(1)}, bf16[4096,1024]{1,0:T(8,128)(2,1)S(1)}, f32[3,1024]{1,0:T(4,128)S(1)}) custom-call(f32[512,1024]{1,0:T(8,128)} %refs_0_.1, f32[512,1024]{1,0:T(8,128)} %refs_1_.1, f32[512,1024]{1,0:T(8,128)} %refs_2_.1, f32[512,1024]{1,0:T(8,128)} %refs_3_.1, f32[512,1024]{1,0:T(8,128)} %refs_4_.1, ...), custom_call_target="tpu_custom_call" | custom-call | tf_op jit(solution)/shard_map/gather/pallas_call | solution.py:278
  114.6 9.1 %write.1 = (bf16[4096,1024]{1,0:T(8,128)(2,1)}, bf16[4096,1024]{1,0:T(8,128)(2,1)}, bf16[4096,1024]{1,0:T(8,128)(2,1)}, f32[1024]{0:T(1024)}, f32[1024]{0:T(1024)}, /*index=5*/f32[1024]{0:T(1024)}) custom-call(bf16[4096,1024]{1,0:T(8,128)(2,1)S(1)} %get-tuple-element.10.a, bf16[4096,1024]{1,0:T(8,128)(2,1)S(1)} %get-tuple-element.11.b, ...), custom_call_target="tpu_custom_call" | custom-call | tf_op jit(solution)/shard_map/write/pallas_call | solution.py:306
